TPU v7x, 32 devices: a whole 2x2x4 slice. The times are simulated.
32 devices in a mesh: dp: 4 (over z), fsdp: 8 (over y, x, core).
Axes of the slice: x: 2, y: 2, z: 4, core: 2. Of those that a mesh axis runs over, the one named last changes fastest.
Arguments:
- hidden: bfloat16 [8192, 4096], P(('dp', 'fsdp')), may hold values from -6 to 6
- queries: bfloat16 [8192, 2048], P(('dp', 'fsdp')), may hold values from -6 to 6
- keys: bfloat16 [8192, 512], P(('dp', 'fsdp')), may hold values from -6 to 6
- target: bfloat16 [8192, 2048], P(('dp', 'fsdp')), may hold values from -6 to 6
- lengths: int32 [32], P(('dp', 'fsdp')), may hold values from 64 to 256
- value_weight_frozen: bfloat16 [4096, 512], P('fsdp'), may hold values from -0.09375 to 0.09375
- adapter_down_map: float32 [4096, 64], P('fsdp'), may hold values from -0.09375 to 0.09375
- adapter_up_map: float32 [64, 512], replicated, may hold values from -0.75 to 0.75
- average_down_map: float32 [4096, 64], P('fsdp'), may hold values from -0.09375 to 0.09375
- average_up_map: float32 [64, 512], replicated, may hold values from -0.75 to 0.75
Outputs:
- down_map_gradient: float32 [4096, 64], P('fsdp')
- up_map_gradient: float32 [64, 512], replicated
- average_down_next: float32 [4096, 64], P('fsdp')
- average_up_next: float32 [64, 512], replicated
- loss: float32 [], replicated
Inputs may be any that keep to these rules, and one draw needn't show every extreme that they name: `lengths`: slots at or past a sequence's length are padding.
All inputs are finite; a program needn't handle non-finite values.
Results may differ from a plain program's by a relative error of at most 0.0049.
Values may be sent and summed in bfloat16 or wider, within the bound.
A program may use at most 64 MiB of HBM per device.

v0:
```python
import math
import jax
import jax.numpy as jnp
from jax import lax
from jax.sharding import PartitionSpec as P

HEADS = 16
KEY_VALUE_HEADS = 4
HEAD_DIM = 128
adapter_scale = 2.0
average_decay = 0.9
learning_rate = 1.0
masked_score = -1e30


def per_device(
    hidden,
    queries,
    keys,
    target,
    lengths,
    value_weight_frozen,
    adapter_down_map,
    adapter_up_map,
    average_down_map,
    average_up_map,
):
    tok_rows = hidden.shape[0]
    group_size = HEADS // KEY_VALUE_HEADS
    seq_length = lengths[0]
    down_factor_slice = adapter_down_map.astype(jnp.bfloat16)
    up_factor_slice = adapter_up_map.astype(jnp.bfloat16)
    columns = hidden
    frozen_value_output = jnp.dot(
        columns,
        lax.all_gather(value_weight_frozen, "fsdp", axis=0, tiled=True),
        preferred_element_type=jnp.float32,
    )
    adapter_hidden = jnp.dot(
        columns,
        lax.all_gather(down_factor_slice, "fsdp", axis=0, tiled=True),
        preferred_element_type=jnp.float32,
    )
    adapter_hidden = adapter_hidden.astype(jnp.bfloat16)
    value_outputs = (
        frozen_value_output
        + adapter_scale
        * jnp.dot(adapter_hidden, up_factor_slice, preferred_element_type=jnp.float32)
    ).astype(jnp.bfloat16)
    position = jnp.arange(tok_rows, dtype=jnp.int32)
    allowed = (position[None, :] <= position[:, None]) & (position[None, :] < seq_length)
    q_heads = queries.reshape(tok_rows, KEY_VALUE_HEADS, group_size, HEAD_DIM)
    k_heads = keys.reshape(tok_rows, KEY_VALUE_HEADS, HEAD_DIM)
    v_heads = value_outputs.reshape(tok_rows, KEY_VALUE_HEADS, HEAD_DIM)
    scores = jnp.einsum(
        "tkgd,skd->kgts", q_heads, k_heads, preferred_element_type=jnp.float32
    ) / math.sqrt(HEAD_DIM)
    scores = jnp.where(allowed, scores, masked_score)
    row_max = jnp.max(scores, axis=-1, keepdims=True)
    weights = jnp.exp(scores - row_max)
    attn_probs = (weights / jnp.sum(weights, axis=-1, keepdims=True)).astype(jnp.bfloat16)
    output = jnp.einsum(
        "kgts,skd->tkgd", attn_probs, v_heads, preferred_element_type=jnp.float32
    ).reshape(tok_rows, HEADS * HEAD_DIM)
    live_rows = (position < seq_length)[:, None]
    differ = jnp.where(live_rows, output - target.astype(jnp.float32), 0.0)
    loss_local = jnp.sum(differ * differ)
    cotangent = differ.astype(jnp.bfloat16).reshape(tok_rows, KEY_VALUE_HEADS, group_size, HEAD_DIM)
    value_grad = jnp.einsum(
        "kgts,tkgd->skd", attn_probs, cotangent, preferred_element_type=jnp.float32
    )
    value_grad = value_grad.reshape(tok_rows, KEY_VALUE_HEADS * HEAD_DIM).astype(jnp.bfloat16)
    latent_grad = lax.dot_general(
        value_grad, up_factor_slice, (((1,), (1,)), ((), ())), preferred_element_type=jnp.float32
    ).astype(jnp.bfloat16)
    up_term = lax.dot_general(
        adapter_hidden, value_grad, (((0,), (0,)), ((), ())), preferred_element_type=jnp.float32
    )
    count_local = seq_length.astype(jnp.float32)
    columns = hidden
    down_map_gradient = lax.psum(
        adapter_scale
        * lax.dot_general(
            columns, latent_grad, (((0,), (0,)), ((), ())), preferred_element_type=jnp.float32
        ),
        "dp",
    )
    down_map_gradient = lax.psum_scatter(down_map_gradient, "fsdp", scatter_dimension=0, tiled=True)
    up_map_gradient, loss_sum, token_grand_count = lax.psum(
        (adapter_scale * up_term, loss_local, count_local), ("dp", "fsdp")
    )
    up_map_gradient = up_map_gradient / token_grand_count
    down_map_gradient = down_map_gradient / token_grand_count
    loss = loss_sum / (2.0 * token_grand_count)
    average_down_next = average_decay * average_down_map + (1.0 - average_decay) * (
        adapter_down_map - learning_rate * down_map_gradient
    )
    average_up_next = average_decay * average_up_map + (1.0 - average_decay) * (
        adapter_up_map - learning_rate * up_map_gradient
    )
    return (down_map_gradient, up_map_gradient, average_down_next, average_up_next, loss)


def solution(mesh):
    placed = (
        P(("dp", "fsdp"), None),
        P(("dp", "fsdp"), None),
        P(("dp", "fsdp"), None),
        P(("dp", "fsdp"), None),
        P(("dp", "fsdp")),
        P("fsdp", None),
        P("fsdp", None),
        P(),
        P("fsdp", None),
        P(),
    )
    return jax.shard_map(
        per_device,
        mesh=mesh,
        in_specs=placed,
        out_specs=(P("fsdp", None), P(), P("fsdp", None), P(), P()),
        check_vma=False,
    )
```

profile of v0, /device:TPU:0, one launch (start us, length us, event | category | flops | bytes accessed | tf_op | source)
XLA Modules:
  0.0 281.5 jit_solution(8382225691264275477)
XLA Ops:
  7.2 0.0 copy-start
  7.2 0.0 copy-start.3
  7.2 0.0 all-gather.2.cloned.1.call-start
  7.2 0.7 all-gather.2.cloned.1.call-update
  7.9 0.0 reduce-scatter.2.cloned.1.call-start
  8.6 1.8 reshape.40
  10.4 1.0 reshape.39
  11.4 0.0 copy-done.3
  11.5 11.3 %all_gather.7 = bf16[4096,64]{0,1:T(8,128)(2,1)S(1)} all-gather(bf16[512,64]{0,1:T(8,128)(2,1)S(1)} %convert_element_type.36), channel_id=1, replica_groups=mesh['dp'=4,'fsdp'=8] {'fsdp'}, dimensions={0}, use_global_device_ids=true | all-gather | bytes 589824 | tf_op jit(solution)/shard_map/all_gather | solution.py:41
  22.8 0.1 fusion.13
  22.9 0.0 copy-done
  22.9 1.4 convolution_convert_fusion.1
  24.3 0.7 fusion.10
  25.0 1.2 fusion.19
  26.3 1.8 divide_convert_fusion
  28.0 0.0 copy-start.1
  28.0 0.0 copy-start.5
  28.0 21.2 %all-gather.2.cloned.1.call-done = bf16[4096,512]{1,0:T(8,128)(2,1)} async-done(((bf16[512,512]{1,0:T(8,128)(2,1)}), bf16[4096,512]{1,0:T(8,128)(2,1)}) %all-gather.2.cloned.1.call-update) | async-done | bytes 4194320 | tf_op jit(solution)/shard_map/all_gather | solution.py:36
  49.2 3.4 %fusion.20 = f32[256,512]{1,0:T(8,128)S(1)} fusion(bf16[256,4096]{1,0:T(8,128)(2,1)S(1)} %copy-done, bf16[4096,512]{1,0:T(8,128)(2,1)} %all-gather.2.cloned.1.call-done), kind=kOutput, calls=%fused_computation.36 | convolution fusion | flops 1073741824 | bytes 6815744 | tf_op jit(solution)/shard_map/dot_general | solution.py:34
  52.7 0.0 copy-done.1
  52.7 0.0 copy-done.5
  52.7 0.3 fusion.8
  52.9 0.1 copy.27
  53.1 3.3 %fusion.21 = f32[4,128,4,256]{3,1,2,0:T(8,128)} fusion(bf16[256,4,128,1]{0,2,3,1:T(8,128)(2,1)S(1)} %bitcast.51, bf16[4,4,256,256]{2,3,1,0:T(8,128)(2,1)} %divide_convert_fusion), kind=kOutput, calls=%fused_computation.37 | convolution fusion | flops 268435456 | bytes 4456448 | tf_op jit(solution)/shard_map/kgts,skd->tkgd/dot_general | solution.py:62
  56.4 0.0 copy-start.2
  56.4 3.0 %copy.19 = f32[256,2048]{1,0:T(8,128)} copy(f32[256,2048]{0,1:T(8,128)} %bitcast.47) | data formatting | bytes 4194304 | tf_op jit(solution)/shard_map/reshape | solution.py:64
  59.5 0.0 copy-done.2
  59.5 3.6 %multiply_reduce_fusion = (f32[]{:T(128)}, bf16[256,2048]{1,0:T(8,128)(2,1)}) fusion(f32[256,2048]{1,0:T(8,128)} %copy.19, bf16[256,2048]{1,0:T(8,128)(2,1)S(1)} %copy-done.2, pred[256]{0:T(512)(128)(4,1)S(1)} %iota_compare_fusion.1), kind=kLoop, calls=%fused_computation.7 | loop fusion | flops 3145727 | bytes 4194564 | tf_op jit(solution)/shard_map/reduce_sum | solution.py:67
  63.1 1.5 copy.30
  64.6 2.4 fusion.9
  67.0 0.0 copy-start.6
  67.0 0.0 copy-start.7
  67.0 0.0 copy-start.4
  67.0 0.0 copy-start.8
  67.0 1.8 fusion.1
  68.9 0.0 reduce-scatter.2.cloned.1.call-update
  68.9 0.0 all-reduce.4.cloned.1.call-start
  68.9 0.0 copy-done.6
  69.0 0.9 convolution_multiply_fusion.2
  69.8 0.0 all-reduce.4.cloned.1.call-update
  69.8 0.0 all-reduce.6.cloned.1.call-start
  69.9 39.5 %all-reduce = (f32[]{:T(128)}, f32[]{:T(128)}) all-reduce(f32[]{:T(128)S(6)} %convert_element_type.47, f32[]{:T(128)} %get-tuple-element.11), channel_id=1, replica_groups=mesh['dp'=4,'fsdp'=8] {'dp','fsdp'}, use_global_device_ids=true, to_apply=%region_4.5 | all-reduce | flops 2 | bytes 16 | tf_op jit(solution)/shard_map/psum | solution.py:89
  110.7 0.0 reduce-scatter.2.cloned.1.call-done
  110.7 0.0 all-reduce.6.cloned.1.call-update
  110.7 125.1 %all-reduce.4.cloned.1.call-done = f32[64,512]{1,0:T(8,128)} async-done(((f32[64,512]{1,0:T(8,128)}), f32[64,512]{1,0:T(8,128)}) %all-reduce.4.cloned.1.call-update) | async-done | bytes 131088 | tf_op jit(solution)/shard_map/psum | solution.py:89
  235.8 0.0 copy-done.7
  235.8 2.2 multiply_add_fusion
  238.0 33.7 %all-reduce.6.cloned.1.call-done = f32[512,64]{0,1:T(8,128)} async-done(((f32[512,64]{0,1:T(8,128)}), f32[512,64]{0,1:T(8,128)}) %all-reduce.6.cloned.1.call-update) | async-done | bytes 131088 | tf_op jit(solution)/shard_map/psum | solution.py:81
  271.7 0.0 copy-done.4
  271.7 0.0 copy-done.8
  271.7 2.2 multiply_add_fusion.1
  (2 shorter events, 0.0 us)
Async XLA Ops:
  7.2 15.8 %copy-start = (bf16[256,4096]{1,0:T(8,128)(2,1)S(1)}, bf16[256,4096]{1,0:T(8,128)(2,1)}, u32[]{:S(2)}) copy-start(bf16[256,4096]{1,0:T(8,128)(2,1)} %param.10) | copy-start | bytes 6291460
  7.2 4.3 %copy-start.3 = (f32[512,64]{0,1:T(8,128)S(1)}, f32[512,64]{0,1:T(8,128)}, u32[]{:S(2)}) copy-start(f32[512,64]{0,1:T(8,128)} %param.16) | copy-start | bytes 393220
  7.2 42.0 %all-gather.2.cloned.1.call-start = ((), (), s32[]{:S(2)}) async-start(), calls=%async_computation.1 | async-start | bytes 4718592 | tf_op jit(solution)/shard_map/all_gather | solution.py:36
  7.9 102.8 %reduce-scatter.2.cloned.1.call-start = ((), (), s32[]{:S(2)}) async-start(), calls=%async_computation.3 | async-start | bytes 1179648 | tf_op jit(solution)/shard_map/reduce_scatter | solution.py:88
  28.0 24.6 %copy-start.1 = (f32[64,512]{1,0:T(8,128)S(1)}, f32[64,512]{1,0:T(8,128)}, u32[]{:S(2)}) copy-start(f32[64,512]{1,0:T(8,128)} %param.17) | copy-start | bytes 393220
  28.0 24.6 %copy-start.5 = (bf16[256,64]{0,1:T(8,128)(2,1)S(1)}, bf16[256,64]{0,1:T(8,128)(2,1)}, u32[]{:S(2)}) copy-start(bf16[256,64]{0,1:T(8,128)(2,1)} %convolution_convert_fusion.1) | copy-start | bytes 98308
  56.4 3.0 %copy-start.2 = (bf16[256,2048]{1,0:T(8,128)(2,1)S(1)}, bf16[256,2048]{1,0:T(8,128)(2,1)}, u32[]{:S(2)}) copy-start(bf16[256,2048]{1,0:T(8,128)(2,1)} %param.13) | copy-start | bytes 3145732
  67.0 2.0 copy-start.6
  67.0 168.8 %copy-start.7 = (f32[64,512]{1,0:T(8,128)S(1)}, f32[64,512]{1,0:T(8,128)}, u32[]{:S(2)}) copy-start(f32[64,512]{1,0:T(8,128)} %param.19) | copy-start | bytes 393220
  67.0 204.7 %copy-start.4 = (f32[512,64]{0,1:T(8,128)S(1)}, f32[512,64]{0,1:T(8,128)}, u32[]{:S(2)}) copy-start(f32[512,64]{0,1:T(8,128)} %param.16) | copy-start | bytes 393220
  67.0 204.7 %copy-start.8 = (f32[512,64]{0,1:T(8,128)S(1)}, f32[512,64]{0,1:T(8,128)}, u32[]{:S(2)}) copy-start(f32[512,64]{0,1:T(8,128)} %param.18) | copy-start | bytes 393220
  68.9 166.9 %all-reduce.4.cloned.1.call-start = ((), (), s32[]{:S(2)}) async-start(), calls=%async_computation.2 | async-start | bytes 262144 | tf_op jit(solution)/shard_map/psum | solution.py:89
  69.8 201.8 %all-reduce.6.cloned.1.call-start = ((), (), s32[]{:S(2)}) async-start(), calls=%async_computation.4 | async-start | bytes 262144 | tf_op jit(solution)/shard_map/psum | solution.py:81
Sparse Core Ops, SparseCore 0:
  9.9 39.2 all-gather.1
  69.0 35.9 reduce-scatter.1
  111.1 124.5 all-reduce.3
  237.9 33.6 all-reduce.5
where the time goes:
time: 282 us
  waiting for transfers between devices  181 us (64%)
  blocking collectives  50.9 us (18%)
  between operations  16.9 us (6%)
  matrix products  14.2 us (5%)
  other arithmetic  11.1 us (4%)
  local copies, waits for them, and re-layouts  7.48 us (3%)
    psum x1, waiting for transfers between devices, per_device(): lax.psum((adapter_scale * up_term, loss_local, count_local), ('dp', 'fsdp'))  125 us
    psum x1, blocking collectives, per_device(): lax.psum((adapter_scale * up_term, loss_local, count_local), ('dp', 'fsdp'))  39.5 us
    psum x1, waiting for transfers between devices, per_device(): lax.psum(adapter_scale * lax.dot_general(columns, latent_grad, (((0,), (0...  33.7 us
    all_gather x1, waiting for transfers between devices, per_device(): lax.all_gather(value_weight_frozen, 'fsdp', axis=0, tiled=True)  21.2 us
    all_gather x1, blocking collectives, per_device(): lax.all_gather(down_factor_slice, 'fsdp', axis=0, tiled=True)  11.3 us
  transfers between devices with their start and end apart: 4, of which 3 were waited for; matrix products, arithmetic and copies ran while one was open for 4% of the time, Pallas kernels for 0%

commit v1 on v0

--- a/solution.py
+++ b/solution.py
@@ -87,7 +87,7 @@
     )
     down_map_gradient = lax.psum_scatter(down_map_gradient, "fsdp", scatter_dimension=0, tiled=True)
     up_map_gradient, loss_sum, token_grand_count = lax.psum(
-        (adapter_scale * up_term, loss_local, count_local), ("dp", "fsdp")
+        lax.psum((adapter_scale * up_term, loss_local, count_local), "fsdp"), "dp"
     )
     up_map_gradient = up_map_gradient / token_grand_count
     down_map_gradient = down_map_gradient / token_grand_count

time: 282 us -> 211 us (0.75)
  waiting for transfers between devices: 181 us -> 123 us
  blocking collectives: 50.9 us -> 37 us
    psum x1, waiting for transfers between devices: 125 us -> 51.6 us  [per_device(): lax.psum((adapter_scale * up_term, loss_local, count_local), 'fsdp')]
    reduce_scatter x1, waiting for transfers between devices: 0.02 us -> 38.6 us  [per_device(): lax.psum_scatter(down_map_gradient, 'fsdp', scatter_dimension=0, tiled=True)]
    psum x1, waiting for transfers between devices: 33.7 us -> 10.9 us  [per_device(): lax.psum(adapter_scale * lax.dot_general(columns, latent_grad, (((0,), (0...]
    psum x1 -> x2, blocking collectives: 39.5 us -> 25.7 us  [the longest x1 13 us: per_device(): lax.psum((adapter_scale * up_term, loss_local, count_local), 'fsdp')]
  transfers between devices with their start and end apart: 4 -> 4, of which waited for: 3 -> 4; matrix products, arithmetic and copies ran while one was open for 4% -> 5% of each run, Pallas kernels for 0% -> 0%
where the time goes in v1:
time: 211 us; the launch traced here: 210 us
  waiting for transfers between devices  123 us (58%)
  blocking collectives  37 us (18%)
  between operations  17 us (8%)
  matrix products  14.2 us (7%)
  other arithmetic  11.3 us (5%)
  local copies, waits for them, and re-layouts  7.48 us (4%)
    psum x1, waiting for transfers between devices, per_device(): lax.psum((adapter_scale * up_term, loss_local, count_local), 'fsdp')  51.6 us
    reduce_scatter x1, waiting for transfers between devices, per_device(): lax.psum_scatter(down_map_gradient, 'fsdp', scatter_dimension=0, tiled=True)  38.6 us
    all_gather x1, waiting for transfers between devices, per_device(): lax.all_gather(value_weight_frozen, 'fsdp', axis=0, tiled=True)  21.2 us
    psum x1, blocking collectives, per_device(): lax.psum((adapter_scale * up_term, loss_local, count_local), 'fsdp')  13 us
    psum x1, blocking collectives, per_device(): lax.psum(lax.psum((adapter_scale * up_term, loss_local, count_local), 'fs...  12.7 us
    all_gather x1, blocking collectives, per_device(): lax.all_gather(down_factor_slice, 'fsdp', axis=0, tiled=True)  11.3 us
    psum x1, waiting for transfers between devices, per_device(): lax.psum(adapter_scale * lax.dot_general(columns, latent_grad, (((0,), (0...  10.9 us
  transfers between devices with their start and end apart: 4, of which 4 were waited for; matrix products, arithmetic and copies ran while one was open for 5% of the time, Pallas kernels for 0%

profile of v1, /device:TPU:0, one launch (start us, length us, event | category | flops | bytes accessed | tf_op | source)
XLA Modules:
  0.0 210.2 jit_solution(2461271701099565733)
XLA Ops:
  7.2 0.0 copy-start
  7.2 0.0 copy-start.3
  7.2 0.0 all-gather.2.cloned.1.call-start
  7.2 0.7 all-gather.2.cloned.1.call-update
  7.9 0.0 all-reduce.6.cloned.1.call-start
  8.6 1.8 reshape.40
  10.4 1.0 reshape.39
  11.4 0.0 copy-done.3
  11.5 11.3 %all_gather.7 = bf16[4096,64]{0,1:T(8,128)(2,1)S(1)} all-gather(bf16[512,64]{0,1:T(8,128)(2,1)S(1)} %convert_element_type.36), channel_id=1, replica_groups=mesh['dp'=4,'fsdp'=8] {'fsdp'}, dimensions={0}, use_global_device_ids=true | all-gather | bytes 589824 | tf_op jit(solution)/shard_map/all_gather | solution.py:41
  22.8 0.1 fusion.13
  22.9 0.0 copy-done
  22.9 1.4 convolution_convert_fusion.1
  24.3 0.7 fusion.10
  25.0 1.2 fusion.19
  26.3 1.8 divide_convert_fusion
  28.0 0.0 copy-start.1
  28.0 0.0 copy-start.5
  28.0 21.2 %all-gather.2.cloned.1.call-done = bf16[4096,512]{1,0:T(8,128)(2,1)} async-done(((bf16[512,512]{1,0:T(8,128)(2,1)}), bf16[4096,512]{1,0:T(8,128)(2,1)}) %all-gather.2.cloned.1.call-update) | async-done | bytes 4194320 | tf_op jit(solution)/shard_map/all_gather | solution.py:36
  49.2 3.4 %fusion.20 = f32[256,512]{1,0:T(8,128)S(1)} fusion(bf16[256,4096]{1,0:T(8,128)(2,1)S(1)} %copy-done, bf16[4096,512]{1,0:T(8,128)(2,1)} %all-gather.2.cloned.1.call-done), kind=kOutput, calls=%fused_computation.36 | convolution fusion | flops 1073741824 | bytes 6815744 | tf_op jit(solution)/shard_map/dot_general | solution.py:34
  52.7 0.0 copy-done.1
  52.7 0.0 copy-done.5
  52.7 0.3 fusion.8
  52.9 0.1 copy.27
  53.1 3.3 %fusion.21 = f32[4,128,4,256]{3,1,2,0:T(8,128)} fusion(bf16[256,4,128,1]{0,2,3,1:T(8,128)(2,1)S(1)} %bitcast.51, bf16[4,4,256,256]{2,3,1,0:T(8,128)(2,1)} %divide_convert_fusion), kind=kOutput, calls=%fused_computation.37 | convolution fusion | flops 268435456 | bytes 4456448 | tf_op jit(solution)/shard_map/kgts,skd->tkgd/dot_general | solution.py:62
  56.4 0.0 copy-start.2
  56.4 3.0 %copy.19 = f32[256,2048]{1,0:T(8,128)} copy(f32[256,2048]{0,1:T(8,128)} %bitcast.47) | data formatting | bytes 4194304 | tf_op jit(solution)/shard_map/reshape | solution.py:64
  59.5 0.0 copy-done.2
  59.5 3.6 %multiply_reduce_fusion = (f32[]{:T(128)}, bf16[256,2048]{1,0:T(8,128)(2,1)}) fusion(f32[256,2048]{1,0:T(8,128)} %copy.19, bf16[256,2048]{1,0:T(8,128)(2,1)S(1)} %copy-done.2, pred[256]{0:T(512)(128)(4,1)S(1)} %iota_compare_fusion.1), kind=kLoop, calls=%fused_computation.7 | loop fusion | flops 3145727 | bytes 4194564 | tf_op jit(solution)/shard_map/reduce_sum | solution.py:67
  63.1 1.5 copy.30
  64.6 0.0 copy-start.6
  64.6 2.4 %fusion.9 = bf16[4,128,256]{2,1,0:T(8,128)(2,1)S(1)} fusion(bf16[256,4,4,128]{0,3,2,1:T(8,128)(2,1)S(1)} %bitcast.48, bf16[4,4,256,256]{2,3,1,0:T(8,128)(2,1)} %divide_convert_fusion), kind=kOutput, calls=%fused_computation.17 | convolution fusion | flops 268566528 | bytes 3407872 | tf_op jit(solution)/shard_map/kgts,tkgd->skd/dot_general | solution.py:69
  67.0 0.0 copy-done.6
  67.0 0.9 convolution_multiply_fusion.2
  67.9 0.0 all-reduce.6.cloned.1.call-update
  67.9 0.0 copy-start.7
  67.9 0.0 copy-start.4
  67.9 0.0 copy-start.8
  67.9 0.0 reduce-scatter.2.cloned.1.call-start
  68.0 1.8 fusion.1
  69.8 0.0 reduce-scatter.2.cloned.1.call-update
  69.9 0.0 all-reduce.8.cloned.1.call-start
  69.9 51.6 %all-reduce.6.cloned.1.call-done = f32[64,512]{1,0:T(8,128)} async-done(((f32[64,512]{1,0:T(8,128)}), f32[64,512]{1,0:T(8,128)}) %all-reduce.6.cloned.1.call-update) | async-done | bytes 131088 | tf_op jit(solution)/shard_map/psum | solution.py:90
  121.5 38.6 %reduce-scatter.2.cloned.1.call-done = f32[512,64]{0,1:T(8,128)} async-done(((f32[4096,64]{0,1:T(8,128)}), f32[512,64]{0,1:T(8,128)}) %reduce-scatter.2.cloned.1.call-update) | async-done | bytes 131088 | tf_op jit(solution)/shard_map/reduce_scatter | solution.py:88
  160.0 0.0 all-reduce.8.cloned.1.call-update
  160.1 13.0 %all-reduce = (f32[]{:T(128)}, f32[]{:T(128)}) all-reduce(f32[]{:T(128)S(6)} %convert_element_type.47, f32[]{:T(128)} %get-tuple-element.15), channel_id=1, replica_groups=mesh['dp'=4,'fsdp'=8] {'fsdp'}, use_global_device_ids=true, to_apply=%region_4.5 | all-reduce | flops 2 | bytes 16 | tf_op jit(solution)/shard_map/psum | solution.py:90
  173.0 12.7 %all-reduce.1 = (f32[]{:T(128)}, f32[]{:T(128)}) all-reduce(f32[]{:T(128)} %get-tuple-element.5, f32[]{:T(128)} %get-tuple-element.6), channel_id=1, replica_groups=mesh['dp'=4,'fsdp'=8] {'dp'}, use_global_device_ids=true, to_apply=%region_5.6 | all-reduce | flops 2 | bytes 16 | tf_op jit(solution)/shard_map/psum | solution.py:89
  187.0 10.9 %all-reduce.8.cloned.1.call-done = (f32[512,64]{0,1:T(8,128)}, f32[64,512]{1,0:T(8,128)}) async-done(((f32[512,64]{0,1:T(8,128)}, f32[64,512]{1,0:T(8,128)}), (f32[512,64]{0,1:T(8,128)}, f32[64,512]{1,0:T(8,128)})) %all-reduce.8.cloned.1.call-update) | async-done | bytes 262160 | tf_op jit(solution)/shard_map/psum | solution.py:81
  198.0 0.0 copy-done.7
  198.0 2.3 %multiply_add_fusion = (f32[64,512]{1,0:T(8,128)}, f32[64,512]{1,0:T(8,128)}) fusion(f32[64,512]{1,0:T(8,128)S(1)} %copy-done.1, f32[64,512]{1,0:T(8,128)S(1)} %copy-done.7, f32[64,512]{1,0:T(8,128)} %get-tuple-element.10, f32[]{:T(128)} %get-tuple-element.7), kind=kLoop, calls=%fused_computation.26 | loop fusion | flops 163840 | bytes 655364 | tf_op jit(solution)/shard_map/add | solution.py:98
  200.2 0.0 copy-done.4
  200.2 0.0 copy-done.8
  200.2 2.3 %multiply_add_fusion.1 = (f32[512,64]{0,1:T(8,128)}, f32[512,64]{0,1:T(8,128)}) fusion(f32[512,64]{0,1:T(8,128)S(1)} %copy-done.4, f32[512,64]{0,1:T(8,128)S(1)} %copy-done.8, f32[512,64]{0,1:T(8,128)} %get-tuple-element.9, f32[]{:T(128)} %get-tuple-element.7), kind=kLoop, calls=%fused_computation.27 | loop fusion | flops 163840 | bytes 655364 | tf_op jit(solution)/shard_map/add | solution.py:95
  (2 shorter events, 0.0 us)
Async XLA Ops:
  7.2 15.8 %copy-start = (bf16[256,4096]{1,0:T(8,128)(2,1)S(1)}, bf16[256,4096]{1,0:T(8,128)(2,1)}, u32[]{:S(2)}) copy-start(bf16[256,4096]{1,0:T(8,128)(2,1)} %param.10) | copy-start | bytes 6291460
  7.2 4.3 %copy-start.3 = (f32[512,64]{0,1:T(8,128)S(1)}, f32[512,64]{0,1:T(8,128)}, u32[]{:S(2)}) copy-start(f32[512,64]{0,1:T(8,128)} %param.16) | copy-start | bytes 393220
  7.2 42.0 %all-gather.2.cloned.1.call-start = ((), (), s32[]{:S(2)}) async-start(), calls=%async_computation.1 | async-start | bytes 4718592 | tf_op jit(solution)/shard_map/all_gather | solution.py:36
  7.9 113.5 %all-reduce.6.cloned.1.call-start = ((), (), s32[]{:S(2)}) async-start(), calls=%async_computation.2 | async-start | bytes 262144 | tf_op jit(solution)/shard_map/psum | solution.py:90
  28.0 24.6 %copy-start.1 = (f32[64,512]{1,0:T(8,128)S(1)}, f32[64,512]{1,0:T(8,128)}, u32[]{:S(2)}) copy-start(f32[64,512]{1,0:T(8,128)} %param.17) | copy-start | bytes 393220
  28.0 24.6 %copy-start.5 = (bf16[256,64]{0,1:T(8,128)(2,1)S(1)}, bf16[256,64]{0,1:T(8,128)(2,1)}, u32[]{:S(2)}) copy-start(bf16[256,64]{0,1:T(8,128)(2,1)} %convolution_convert_fusion.1) | copy-start | bytes 98308
  56.4 3.0 %copy-start.2 = (bf16[256,2048]{1,0:T(8,128)(2,1)S(1)}, bf16[256,2048]{1,0:T(8,128)(2,1)}, u32[]{:S(2)}) copy-start(bf16[256,2048]{1,0:T(8,128)(2,1)} %param.13) | copy-start | bytes 3145732
  64.6 2.4 %copy-start.6 = (bf16[256,64]{0,1:T(8,128)(2,1)S(1)}, bf16[256,64]{0,1:T(8,128)(2,1)}, u32[]{:S(2)}) copy-start(bf16[256,64]{0,1:T(8,128)(2,1)} %convolution_convert_fusion.1) | copy-start | bytes 98308
  67.9 130.1 %copy-start.7 = (f32[64,512]{1,0:T(8,128)S(1)}, f32[64,512]{1,0:T(8,128)}, u32[]{:S(2)}) copy-start(f32[64,512]{1,0:T(8,128)} %param.19) | copy-start | bytes 393220
  67.9 132.3 %copy-start.4 = (f32[512,64]{0,1:T(8,128)S(1)}, f32[512,64]{0,1:T(8,128)}, u32[]{:S(2)}) copy-start(f32[512,64]{0,1:T(8,128)} %param.16) | copy-start | bytes 393220
  67.9 132.3 %copy-start.8 = (f32[512,64]{0,1:T(8,128)S(1)}, f32[512,64]{0,1:T(8,128)}, u32[]{:S(2)}) copy-start(f32[512,64]{0,1:T(8,128)} %param.18) | copy-start | bytes 393220
  67.9 92.1 %reduce-scatter.2.cloned.1.call-start = ((), (), s32[]{:S(2)}) async-start(), calls=%async_computation.3 | async-start | bytes 1179648 | tf_op jit(solution)/shard_map/reduce_scatter | solution.py:88
  69.9 128.1 %all-reduce.8.cloned.1.call-start = ((), (), s32[]{:S(2)}) async-start(), calls=%async_computation.4 | async-start | bytes 524288 | tf_op jit(solution)/shard_map/psum | solution.py:81
Sparse Core Ops, SparseCore 0:
  9.9 39.2 all-gather.1
  68.0 53.4 all-reduce.5
  124.7 35.3 reduce-scatter.1
  162.3 35.6 all-reduce.7
